TPU v7x, 32 devices: a whole 2x2x4 slice. The times are simulated.
32 devices in a mesh: pb: 4 (over z), ka: 8 (over y, x, core).
Axes of the slice: x: 2, y: 2, z: 4, core: 2. Of those that a mesh axis runs over, the one named last changes fastest.
Arguments:
- queries: float32 [1, 4096, 128], P(None, ('pb', 'ka')), may hold values from -6 to 6
- keys: float32 [1, 4096, 128], P(None, ('ka', 'pb')), may hold values from -6 to 6
- values: float32 [1, 4096, 128], P(None, ('ka', 'pb')), may hold values from -6 to 6
- tangent_q: float32 [1, 4096, 128], P(None, ('pb', 'ka')), may hold values from -6 to 6
- tangent_k: float32 [1, 4096, 128], P(None, ('ka', 'pb')), may hold values from -6 to 6
- tangent_v: float32 [1, 4096, 128], P(None, ('ka', 'pb')), may hold values from -6 to 6
Outputs:
- attended: float32 [1, 4096, 128], P(None, ('pb', 'ka'))
- attended_tangent: float32 [1, 4096, 128], P(None, ('pb', 'ka'))
All inputs are finite; a program needn't handle non-finite values.
Results may differ from a plain program's by a relative error of at most 0.0003.
Values sent between devices are 32-bit elements; how exact they have to be, the bound alone decides.
No kernel may reach another device: no remote copies, remote signals or barrier semaphores. Data moves between devices by JAX's collectives and lax.ppermute only.
A program may use at most 128 MiB of HBM per device.

v0:
```python
import jax
import jax.numpy as jnp
from jax import lax
from jax.sharding import PartitionSpec as P


def combined_all(value, axis, join):
    pieces = jax.tree.map(lambda part: lax.all_gather(part, axis), value)
    head = jax.tree.map(lambda part: part[0], pieces)
    tail = jax.tree.map(lambda part: part[1:], pieces)
    so_far, _ = lax.scan(lambda so_far, share: (join(so_far, share), None), head, tail)
    return so_far


def join_partials(first, second):
    peak = jnp.maximum(first[0], second[0])
    left = jnp.exp(first[0] - peak)
    right = jnp.exp(second[0] - peak)
    total = first[1] * left + second[1] * right
    numer = first[2] * left[..., None] + second[2] * right[..., None]
    tnumer = first[3] * left[..., None] + second[3] * right[..., None]
    drift = first[4] * left + second[4] * right
    return (peak, total, numer, tnumer, drift)


def body(queries, keys, values, tangent_q, tangent_k, tangent_v):
    highest = lax.Precision.HIGHEST
    head_count, _, width = queries.shape
    factor = width ** (-0.5)
    all_q, all_dq = (
        lax.all_gather(queries, "ka", axis=1, tiled=True),
        lax.all_gather(tangent_q, "ka", axis=1, tiled=True),
    )
    span = all_q.shape[1]
    block = min(512, span)
    blocks = span // block
    split_q = all_q.reshape(head_count, blocks, block, width)
    split_dq = all_dq.reshape(head_count, blocks, block, width)
    start_state = (
        jnp.full((head_count, span), -1e30, jnp.float32),
        jnp.zeros((head_count, span), jnp.float32),
        jnp.zeros((head_count, span, width), jnp.float32),
        jnp.zeros((head_count, span, width), jnp.float32),
        jnp.zeros((head_count, span), jnp.float32),
    )
    piece_k = lax.all_gather(keys, "pb", axis=1, tiled=True)
    piece_dk = lax.all_gather(tangent_k, "pb", axis=1, tiled=True)
    piece_v = lax.all_gather(values, "pb", axis=1, tiled=True)
    piece_dv = lax.all_gather(tangent_v, "pb", axis=1, tiled=True)
    shaped = (
        start_state[0].reshape(head_count, blocks, block),
        start_state[1].reshape(head_count, blocks, block),
        start_state[2].reshape(head_count, blocks, block, width),
        start_state[3].reshape(head_count, blocks, block, width),
        start_state[4].reshape(head_count, blocks, block),
    )

    def one_head(items):
        (
            head_q,
            head_dq,
            head_k,
            head_dk,
            head_v,
            head_dv,
            peak_h,
            total_h,
            numer_h,
            tnumer_h,
            drift_h,
        ) = items

        def one_block(parts):
            query_blk, dquery_blk, old_peak, old_total, old_numer, old_tnumer, old_drift = parts
            scores = jnp.dot(query_blk, head_k.T, precision=highest) * factor
            tangent = (
                jnp.dot(dquery_blk, head_k.T, precision=highest)
                + jnp.dot(query_blk, head_dk.T, precision=highest)
            ) * factor
            new_peak = jnp.maximum(old_peak, jnp.max(scores, axis=1))
            rescale = jnp.exp(old_peak - new_peak)
            weights = jnp.exp(scores - new_peak[:, None])
            product = weights * tangent
            new_total = old_total * rescale + jnp.sum(weights, axis=1)
            new_numer = old_numer * rescale[:, None] + jnp.dot(weights, head_v, precision=highest)
            new_tnumer = (
                old_tnumer * rescale[:, None]
                + jnp.dot(weights, head_dv, precision=highest)
                + jnp.dot(product, head_v, precision=highest)
            )
            new_drift = old_drift * rescale + jnp.sum(product, axis=1)
            return (new_peak, new_total, new_numer, new_tnumer, new_drift)

        return lax.map(one_block, (head_q, head_dq, peak_h, total_h, numer_h, tnumer_h, drift_h))

    result = lax.map(one_head, (split_q, split_dq, piece_k, piece_dk, piece_v, piece_dv) + shaped)
    peak = result[0].reshape(head_count, span)
    total = result[1].reshape(head_count, span)
    numer = result[2].reshape(head_count, span, width)
    tnumer = result[3].reshape(head_count, span, width)
    drift = result[4].reshape(head_count, span)
    merged = combined_all((peak, total, numer, tnumer, drift), "ka", join_partials)
    owned = span // lax.axis_size("ka")
    offset = lax.axis_index("ka") * owned
    total = lax.dynamic_slice_in_dim(merged[1], offset, owned, 1)
    numer = lax.dynamic_slice_in_dim(merged[2], offset, owned, 1)
    tnumer = lax.dynamic_slice_in_dim(merged[3], offset, owned, 1)
    drift = lax.dynamic_slice_in_dim(merged[4], offset, owned, 1)
    attended = numer / total[..., None]
    attended_tangent = tnumer / total[..., None] - attended * (drift / total)[..., None]
    return (attended, attended_tangent)


def solution(mesh):
    return jax.shard_map(
        body,
        mesh=mesh,
        in_specs=(
            P(None, ("pb", "ka"), None),
            P(None, ("ka", "pb"), None),
            P(None, ("ka", "pb"), None),
            P(None, ("pb", "ka"), None),
            P(None, ("ka", "pb"), None),
            P(None, ("ka", "pb"), None),
        ),
        out_specs=(P(None, ("pb", "ka"), None), P(None, ("pb", "ka"), None)),
        check_vma=False,
    )
```

profile of v0, /device:TPU:0, one launch (start us, length us, event | category | flops | bytes accessed | tf_op | source)
XLA Modules:
  0.0 214.0 jit_solution(3527905628978141757)
XLA Ops:
  7.2 0.0 all-gather.5.cloned.1.call-start
  7.3 15.9 %all_gather.34 = f32[1,512,128]{2,1,0:T(8,128)S(1)} all-gather(f32[1,128,128]{2,1,0:T(8,128)} %param.11), channel_id=1, replica_groups=mesh['pb'=4,'ka'=8] {'pb'}, dimensions={1}, use_global_device_ids=true | all-gather | bytes 327680 | tf_op jit(solution)/shard_map/all_gather | solution.py:46
  23.1 14.9 %all_gather.35 = f32[1,512,128]{2,1,0:T(8,128)S(1)} all-gather(f32[1,128,128]{2,1,0:T(8,128)} %param.12), channel_id=1, replica_groups=mesh['pb'=4,'ka'=8] {'pb'}, dimensions={1}, use_global_device_ids=true | all-gather | bytes 327680 | tf_op jit(solution)/shard_map/all_gather | solution.py:48
  38.0 14.0 %all_gather.38 = f32[1,512,128]{2,1,0:T(8,128)S(1)} all-gather(f32[1,128,128]{2,1,0:T(8,128)} %param.14), channel_id=1, replica_groups=mesh['pb'=4,'ka'=8] {'pb'}, dimensions={1}, use_global_device_ids=true | all-gather | bytes 327680 | tf_op jit(solution)/shard_map/all_gather | solution.py:47
  52.1 16.6 %all_gather.36 = f32[1,512,128]{2,1,0:T(8,128)} all-gather(f32[1,128,128]{2,1,0:T(8,128)} %param.15), channel_id=1, replica_groups=mesh['pb'=4,'ka'=8] {'pb'}, dimensions={1}, use_global_device_ids=true | all-gather | bytes 327680 | tf_op jit(solution)/shard_map/all_gather | solution.py:49
  68.6 10.1 %all_gather.33 = f32[1,1024,128]{2,1,0:T(8,128)S(1)} all-gather(f32[1,128,128]{2,1,0:T(8,128)} %param.10), channel_id=1, replica_groups=mesh['pb'=4,'ka'=8] {'ka'}, dimensions={1}, use_global_device_ids=true | all-gather | bytes 589824 | tf_op jit(solution)/shard_map/all_gather | solution.py:31
  78.8 10.8 %all_gather.37 = f32[1,1024,128]{2,1,0:T(8,128)} all-gather(f32[1,128,128]{2,1,0:T(8,128)} %param.13), channel_id=1, replica_groups=mesh['pb'=4,'ka'=8] {'ka'}, dimensions={1}, use_global_device_ids=true | all-gather | bytes 589824 | tf_op jit(solution)/shard_map/all_gather | solution.py:32
  89.5 24.6 %while.53 = (s32[]{:T(128)}, f32[2,512]{1,0:T(2,128)S(1)}, f32[2,512]{1,0:T(2,128)S(1)}, f32[2,512,128]{2,1,0:T(8,128)}, f32[2,512,128]{2,1,0:T(8,128)}, /*index...) while((s32[]{:T(128)}, f32[2,512]{1,0:T(2,128)S(1)}, ...), condition=%wide.region_4.5_spmd, body=%wide.region_0.4_spmd.sunk | while | flops 2419001344 | bytes 12892333 | solution.py:94
  89.5 1.9 fusion.66
  91.5 1.0 fusion.65
  92.5 0.2 fusion.68
  92.7 1.2 fusion.67
  94.0 2.8 %convolution_add_fusion.5 = f32[512,128]{1,0:T(8,128)S(1)} fusion(f32[512,128]{1,0:T(8,128)} %get-tuple-element.549, f32[512,512]{0,1:T(8,128)S(1)} %get-tuple-element.489, f32[512]{0:T(512)S(1)} %get-tuple-element.488, f32[512]{0:T(512)S(1)} %get-tuple-element.492), kind=kOutput, calls=%fused_computation.7.clone.1 | convolution fusion | flops 402980864 | bytes 1576960 | tf_op jit(solution)/shard_map/while/body/eval_jaxpr/while/body/eval_jaxpr/dot_general | solution.py:88
  96.8 2.5 %fusion.71 = f32[2,512,128]{2,1,0:T(8,128)} fusion(f32[2,512,128]{2,1,0:T(8,128)} %get-tuple-element.530, s32[]{:T(128)S(6)} %copy.19, f32[512,128]{1,0:T(8,128)S(1)} %convolution_add_fusion.5, f32[512,512]{0,1:T(8,128)S(1)} %get-tuple-element.493, f32[512,128]{1,0:T(8,128)S(1)} %get-tuple-element.548), kind=kOutput, calls=%fused_computation.6.clone.1 | convolution fusion | flops 402718720 | bytes 1835012 | tf_op jit(solution)/shard_map/while/body/eval_jaxpr/while/body/eval_jaxpr/dot_general | solution.py:89
  99.3 2.5 %fusion.70 = f32[2,512,128]{2,1,0:T(8,128)} fusion(f32[2,512,128]{2,1,0:T(8,128)} %get-tuple-element.529, s32[]{:T(128)S(6)} %copy.19, f32[512,128]{1,0:T(8,128)S(1)} %get-tuple-element.548, f32[512,512]{0,1:T(8,128)S(1)} %get-tuple-element.489, f32[512]{0:T(512)S(1)} %get-tuple-element.488, f32[512]{0:T(512)S(1)} %get-tuple-element.492), kind=kOutput, calls=%fused_computation.10.clone.1 | convolution fusion | flops 402980864 | bytes 1576964 | tf_op jit(solution)/shard_map/while/body/eval_jaxpr/while/body/eval_jaxpr/dot_general | solution.py:85
  101.9 1.9 fusion.66
  103.8 1.0 fusion.65
  104.9 0.2 fusion.68
  105.1 1.2 fusion.67
  106.4 2.8 %convolution_add_fusion.5 = f32[512,128]{1,0:T(8,128)S(1)} fusion(f32[512,128]{1,0:T(8,128)} %get-tuple-element.549, f32[512,512]{0,1:T(8,128)S(1)} %get-tuple-element.489, f32[512]{0:T(512)S(1)} %get-tuple-element.488, f32[512]{0:T(512)S(1)} %get-tuple-element.492), kind=kOutput, calls=%fused_computation.7.clone.1 | convolution fusion | flops 402980864 | bytes 1576960 | tf_op jit(solution)/shard_map/while/body/eval_jaxpr/while/body/eval_jaxpr/dot_general | solution.py:88
  109.1 2.5 %fusion.71 = f32[2,512,128]{2,1,0:T(8,128)} fusion(f32[2,512,128]{2,1,0:T(8,128)} %get-tuple-element.530, s32[]{:T(128)S(6)} %copy.19, f32[512,128]{1,0:T(8,128)S(1)} %convolution_add_fusion.5, f32[512,512]{0,1:T(8,128)S(1)} %get-tuple-element.493, f32[512,128]{1,0:T(8,128)S(1)} %get-tuple-element.548), kind=kOutput, calls=%fused_computation.6.clone.1 | convolution fusion | flops 402718720 | bytes 1835012 | tf_op jit(solution)/shard_map/while/body/eval_jaxpr/while/body/eval_jaxpr/dot_general | solution.py:89
  111.7 2.5 %fusion.70 = f32[2,512,128]{2,1,0:T(8,128)} fusion(f32[2,512,128]{2,1,0:T(8,128)} %get-tuple-element.529, s32[]{:T(128)S(6)} %copy.19, f32[512,128]{1,0:T(8,128)S(1)} %get-tuple-element.548, f32[512,512]{0,1:T(8,128)S(1)} %get-tuple-element.489, f32[512]{0:T(512)S(1)} %get-tuple-element.488, f32[512]{0:T(512)S(1)} %get-tuple-element.492), kind=kOutput, calls=%fused_computation.10.clone.1 | convolution fusion | flops 402980864 | bytes 1576964 | tf_op jit(solution)/shard_map/while/body/eval_jaxpr/while/body/eval_jaxpr/dot_general | solution.py:85
  114.2 0.0 all-gather.5.cloned.1.call-update
  114.2 0.0 all-gather.3.cloned.1.call-start
  114.3 0.7 all-gather.3.cloned.1.call-update
  115.0 8.8 %all_gather.40 = f32[8,1,1024]{2,1,0:T(1,128)S(1)} all-gather(f32[1,1,1024]{2,1,0:T(1,128)S(1)} %all_gather_reshape.16), channel_id=1, replica_groups=mesh['pb'=4,'ka'=8] {'ka'}, dimensions={0}, use_global_device_ids=true | all-gather | bytes 36864 | tf_op jit(solution)/shard_map/all_gather | solution.py:8
  123.8 0.0 copy-start
  123.8 8.6 %all_gather.39 = f32[8,1,1024]{2,1,0:T(1,128)S(1)} all-gather(f32[1,1,1024]{2,1,0:T(1,128)S(1)} %all_gather_reshape.15), channel_id=1, replica_groups=mesh['pb'=4,'ka'=8] {'ka'}, dimensions={0}, use_global_device_ids=true | all-gather | bytes 36864 | tf_op jit(solution)/shard_map/all_gather | solution.py:8
  132.4 0.0 copy-start.1
  132.4 9.0 %all_gather.43 = f32[8,1,1024]{2,1,0:T(1,128)S(1)} all-gather(f32[1,1,1024]{2,1,0:T(1,128)S(1)} %all_gather_reshape.19), channel_id=1, replica_groups=mesh['pb'=4,'ka'=8] {'ka'}, dimensions={0}, use_global_device_ids=true | all-gather | bytes 36864 | tf_op jit(solution)/shard_map/all_gather | solution.py:8
  141.4 0.0 copy-start.2
  141.4 8.8 %all-gather.5.cloned.1.call-done = f32[8,1,1024,128]{3,2,1,0:T(8,128)} async-done(((f32[1,1,1024,128]{3,2,1,0:T(8,128)}), f32[8,1,1024,128]{3,2,1,0:T(8,128)}) %all-gather.5.cloned.1.call-update) | async-done | bytes 4194320 | tf_op jit(solution)/shard_map/all_gather | solution.py:8
  150.2 4.1 %slice.48 = f32[7,1,1024,128]{3,2,1,0:T(8,128)} slice(f32[8,1,1024,128]{3,2,1,0:T(8,128)} %all-gather.5.cloned.1.call-done), slice={[1:8], [0:1], [0:1024], [0:128]} | slice | bytes 7340032 | tf_op jit(solution)/shard_map/slice | solution.py:10
  154.3 1.1 slice_bitcast_fusion
  155.3 0.0 copy-done
  155.4 0.0 copy-done.1
  155.4 0.0 copy-done.2
  155.4 33.3 %all-gather.3.cloned.1.call-done = f32[8,1,1024,128]{3,2,1,0:T(8,128)} async-done(((f32[1,1,1024,128]{3,2,1,0:T(8,128)}), f32[8,1,1024,128]{3,2,1,0:T(8,128)}) %all-gather.3.cloned.1.call-update) | async-done | bytes 4194320 | tf_op jit(solution)/shard_map/all_gather | solution.py:8
  188.7 0.0 slice-start
  188.7 0.0 slice-start.1
  188.7 0.0 slice-start.2
  188.7 1.1 slice_bitcast_fusion.1
  189.8 4.1 %slice.47 = f32[7,1,1024,128]{3,2,1,0:T(8,128)} slice(f32[8,1,1024,128]{3,2,1,0:T(8,128)} %all-gather.3.cloned.1.call-done), slice={[1:8], [0:1], [0:1024], [0:128]} | slice | bytes 7340032 | tf_op jit(solution)/shard_map/slice | solution.py:10
  193.8 0.0 slice-done
  193.8 0.0 slice-done.1
  193.8 0.0 slice-done.2
  193.8 12.5 %while.54 = (s32[]{:T(128)}, f32[1,1024]{1,0:T(1,128)S(1)}, f32[1,1024]{1,0:T(1,128)S(1)}, f32[1,1024,128]{2,1,0:T(8,128)S(1)}, f32[1,1024,128]{2,1,0:T(8,128)S(...) while((s32[]{:T(128)}, f32[1,1024]{1,0:T(1,128)S(1)}, ...), condition=%wide.region_6.7_spmd, body=%wide.region_5.6_spmd.sunk | while | flops 795650 | bytes 3207305 | solution.py:11
  193.9 1.7 fusion.74
  195.7 1.7 fusion.74
  197.5 1.7 fusion.74
  199.3 1.7 fusion.74
  201.1 1.7 fusion.74
  202.9 1.7 fusion.74
  204.7 1.7 fusion.74
  206.4 0.7 multiply_subtract_fusion
  (36 shorter events, 0.8 us)
Async XLA Ops:
  7.2 143.0 %all-gather.5.cloned.1.call-start = ((), (), s32[]{:S(2)}) async-start(), calls=%async_computation.1 | async-start | bytes 4718592 | tf_op jit(solution)/shard_map/all_gather | solution.py:8
  114.2 74.5 %all-gather.3.cloned.1.call-start = ((), (), s32[]{:S(2)}) async-start(), calls=%async_computation | async-start | bytes 4718592 | tf_op jit(solution)/shard_map/all_gather | solution.py:8
  123.8 31.5 %copy-start = (f32[8,1,1024]{2,1,0:T(1,128)}, f32[8,1,1024]{2,1,0:T(1,128)S(1)}, u32[]{:S(2)}) copy-start(f32[8,1,1024]{2,1,0:T(1,128)S(1)} %all_gather.40) | copy-start | bytes 98308
  132.4 22.9 %copy-start.1 = (f32[8,1,1024]{2,1,0:T(1,128)}, f32[8,1,1024]{2,1,0:T(1,128)S(1)}, u32[]{:S(2)}) copy-start(f32[8,1,1024]{2,1,0:T(1,128)S(1)} %all_gather.39) | copy-start | bytes 98308
  141.4 13.9 %copy-start.2 = (f32[8,1,1024]{2,1,0:T(1,128)}, f32[8,1,1024]{2,1,0:T(1,128)S(1)}, u32[]{:S(2)}) copy-start(f32[8,1,1024]{2,1,0:T(1,128)S(1)} %all_gather.43) | copy-start | bytes 98308
  188.7 5.2 %slice-start = ((f32[8,1,1024]{2,1,0:T(1,128)}), f32[7,1,1024]{2,1,0:T(1,128)S(1)}, s32[]{:S(2)}) async-start(f32[8,1,1024]{2,1,0:T(1,128)} %copy-done), calls=%async_computation.2 | async-start | bytes 57344 | tf_op jit(solution)/shard_map/slice | solution.py:10
  188.7 5.2 %slice-start.1 = ((f32[8,1,1024]{2,1,0:T(1,128)}), f32[7,1,1024]{2,1,0:T(1,128)S(1)}, s32[]{:S(2)}) async-start(f32[8,1,1024]{2,1,0:T(1,128)} %copy-done.1), calls=%async_computation.3 | async-start | bytes 57344 | tf_op jit(solution)/shard_map/slice | solution.py:10
  188.7 5.2 %slice-start.2 = ((f32[8,1,1024]{2,1,0:T(1,128)}), f32[7,1,1024]{2,1,0:T(1,128)S(1)}, s32[]{:S(2)}) async-start(f32[8,1,1024]{2,1,0:T(1,128)} %copy-done.2), calls=%async_computation.4 | async-start | bytes 57344 | tf_op jit(solution)/shard_map/slice | solution.py:10
Sparse Core Ops, SparseCore 0:
  114.3 35.8 all-gather.4
  152.1 36.5 all-gather.2
where the time goes:
time: 215 us; the launch traced here: 214 us
  blocking collectives  109 us (51%)
  waiting for transfers between devices  42.8 us (20%)
  matrix products  23.9 us (11%)
  between operations  14.1 us (7%)
  other arithmetic  13.6 us (6%)
  local copies, waits for them, and re-layouts  10.6 us (5%)
    all_gather x2, waiting for transfers between devices, combined_all(): pieces = jax.tree.map(lambda part: lax.all_gather(part, axis), value)  42.1 us
    all_gather x3, blocking collectives, combined_all(): pieces = jax.tree.map(lambda part: lax.all_gather(part, axis), value)  26.4 us
    all_gather x1, blocking collectives, body(): piece_dv = lax.all_gather(tangent_v, 'pb', axis=1, tiled=True)  16.6 us
    all_gather x1, blocking collectives, body(): piece_k = lax.all_gather(keys, 'pb', axis=1, tiled=True)  15.9 us
    all_gather x1, blocking collectives, body(): piece_v = lax.all_gather(values, 'pb', axis=1, tiled=True)  14.9 us
    all_gather x1, blocking collectives, body(): piece_dk = lax.all_gather(tangent_k, 'pb', axis=1, tiled=True)  14 us
    add x7, other arithmetic, join_partials(): tnumer = first[3] * left[..., None] + second[3] * right[..., None]  11.9 us
    all_gather x1, blocking collectives, body(): lax.all_gather(tangent_q, 'ka', axis=1, tiled=True)  10.8 us
  transfers between devices with their start and end apart: 2, of which 2 were waited for; matrix products, arithmetic and copies ran while one was open for 2% of the time, Pallas kernels for 0%

commit v1 on v0

--- a/solution.py
+++ b/solution.py
@@ -45,7 +45,18 @@
     )
     piece_k = lax.all_gather(keys, "pb", axis=1, tiled=True)
     piece_dk = lax.all_gather(tangent_k, "pb", axis=1, tiled=True)
-    piece_v = lax.all_gather(values, "pb", axis=1, tiled=True)
+    full_n = jax.lax.axis_size("pb")
+    slots = [values]
+    to_i = 0
+    while to_i < full_n - 1:
+        slots.append(
+            jax.lax.ppermute(
+                slots[-1], axis_name="pb", perm=[(num, (num + 1) % full_n) for num in range(full_n)]
+            )
+        )
+        to_i = to_i + 1
+    state_next = jnp.concatenate(slots[::-1], axis=1)
+    piece_v = jnp.roll(state_next, (jax.lax.axis_index("pb") + 1) * values.shape[1], axis=1)
     piece_dv = lax.all_gather(tangent_v, "pb", axis=1, tiled=True)
     shaped = (
         start_state[0].reshape(head_count, blocks, block),

time: 215 us -> 204 us (0.949)
  blocking collectives: 109 us -> 92.2 us
  starting transfers between devices: 0.08 us -> 4.44 us
    all_gather x1 -> x0, blocking collectives: 14.9 us -> none  [body(): piece_v = lax.all_gather(values, 'pb', axis=1, tiled=True)]
    ppermute x0 -> x3, starting transfers between devices: none -> 4.37 us  [body(): jax.lax.ppermute(slots[-1], axis_name='pb', perm=[(num, (num + 1) % full_...]
  transfers between devices with their start and end apart: 2 -> 5, of which waited for: 2 -> 2; matrix products, arithmetic and copies ran while one was open for 2% -> 3% of each run, Pallas kernels for 0% -> 0%
where the time goes in v1:
time: 204 us; the launch traced here: 203 us
  blocking collectives  92.2 us (45%)
  waiting for transfers between devices  42.4 us (21%)
  matrix products  23.9 us (12%)
  between operations  14.2 us (7%)
  other arithmetic  13.6 us (7%)
  local copies, waits for them, and re-layouts  12.4 us (6%)
  starting transfers between devices  4.44 us (2%)
    all_gather x2, waiting for transfers between devices, combined_all(): pieces = jax.tree.map(lambda part: lax.all_gather(part, axis), value)  41.7 us
    all_gather x3, blocking collectives, combined_all(): pieces = jax.tree.map(lambda part: lax.all_gather(part, axis), value)  26.4 us
    all_gather x1, blocking collectives, body(): piece_dv = lax.all_gather(tangent_v, 'pb', axis=1, tiled=True)  15.8 us
    all_gather x1, blocking collectives, body(): piece_dk = lax.all_gather(tangent_k, 'pb', axis=1, tiled=True)  14.9 us
    all_gather x1, blocking collectives, body(): piece_k = lax.all_gather(keys, 'pb', axis=1, tiled=True)  14.3 us
    add x7, other arithmetic, join_partials(): tnumer = first[3] * left[..., None] + second[3] * right[..., None]  11.9 us
    all_gather x1, blocking collectives, body(): lax.all_gather(tangent_q, 'ka', axis=1, tiled=True)  10.8 us
    all_gather x1, blocking collectives, body(): lax.all_gather(queries, 'ka', axis=1, tiled=True)  10.1 us
  transfers between devices with their start and end apart: 5, of which 2 were waited for; matrix products, arithmetic and copies ran while one was open for 3% of the time, Pallas kernels for 0%

profile of v1, /device:TPU:0, one launch (start us, length us, event | category | flops | bytes accessed | tf_op | source)
XLA Modules:
  0.0 203.3 jit_solution(11453829202141541786)
XLA Ops:
  7.2 0.0 all-gather.5.cloned.1.call-start
  7.2 3.1 %collective-permute-start = (f32[1,128,128]{2,1,0:T(8,128)}, f32[1,128,128]{2,1,0:T(8,128)S(1)}, u32[]{:S(2)}, u32[]{:S(2)}) collective-permute-start(f32[1,128,128]{2,1,0:T(8,128)} %param.12), channel_id=1, source_target_pairs={{0,8},{8,16},{16,24},{24,0},{1,9},{9,17},{17,25},{25,1},{2,10},{10... | collective-permute-start | bytes 196616 | tf_op jit(solution)/shard_map/ppermute | solution.py:53
  10.3 10.1 %all_gather.30 = f32[1,1024,128]{2,1,0:T(8,128)S(1)} all-gather(f32[1,128,128]{2,1,0:T(8,128)} %param.10), channel_id=1, replica_groups=mesh['pb'=4,'ka'=8] {'ka'}, dimensions={1}, use_global_device_ids=true | all-gather | bytes 589824 | tf_op jit(solution)/shard_map/all_gather | solution.py:31
  20.5 10.8 %all_gather.33 = f32[1,1024,128]{2,1,0:T(8,128)} all-gather(f32[1,128,128]{2,1,0:T(8,128)} %param.13), channel_id=1, replica_groups=mesh['pb'=4,'ka'=8] {'ka'}, dimensions={1}, use_global_device_ids=true | all-gather | bytes 589824 | tf_op jit(solution)/shard_map/all_gather | solution.py:32
  31.2 14.3 %all_gather.31 = f32[1,512,128]{2,1,0:T(8,128)S(1)} all-gather(f32[1,128,128]{2,1,0:T(8,128)} %param.11), channel_id=1, replica_groups=mesh['pb'=4,'ka'=8] {'pb'}, dimensions={1}, use_global_device_ids=true | all-gather | bytes 327680 | tf_op jit(solution)/shard_map/all_gather | solution.py:46
  45.5 0.0 collective-permute-done
  45.5 0.2 collective-permute-start.1
  45.8 14.9 %all_gather.34 = f32[1,512,128]{2,1,0:T(8,128)S(1)} all-gather(f32[1,128,128]{2,1,0:T(8,128)} %param.14), channel_id=1, replica_groups=mesh['pb'=4,'ka'=8] {'pb'}, dimensions={1}, use_global_device_ids=true | all-gather | bytes 327680 | tf_op jit(solution)/shard_map/all_gather | solution.py:47
  60.6 0.0 collective-permute-done.1
  60.6 1.0 collective-permute-start.2
  61.6 15.8 %all_gather.32 = f32[1,512,128]{2,1,0:T(8,128)} all-gather(f32[1,128,128]{2,1,0:T(8,128)} %param.15), channel_id=1, replica_groups=mesh['pb'=4,'ka'=8] {'pb'}, dimensions={1}, use_global_device_ids=true | all-gather | bytes 327680 | tf_op jit(solution)/shard_map/all_gather | solution.py:60
  77.4 0.0 collective-permute-done.2
  77.5 0.8 constant_dynamic-update-slice_fusion.4
  78.3 0.8 constant_dynamic-update-slice_fusion
  79.2 24.6 %while.53 = (s32[]{:T(128)}, f32[2,512]{1,0:T(2,128)S(1)}, f32[2,512]{1,0:T(2,128)S(1)}, f32[2,512,128]{2,1,0:T(8,128)}, f32[2,512,128]{2,1,0:T(8,128)}, /*index...) while((s32[]{:T(128)}, f32[2,512]{1,0:T(2,128)S(1)}, ...), condition=%wide.region_4.5_spmd, body=%wide.region_0.4_spmd.sunk | while | flops 2419001344 | bytes 12892333 | solution.py:105
  79.2 1.9 fusion.66
  81.2 1.0 fusion.65
  82.2 0.2 fusion.68
  82.4 1.2 fusion.67
  83.7 2.8 %convolution_add_fusion.5 = f32[512,128]{1,0:T(8,128)S(1)} fusion(f32[512,128]{1,0:T(8,128)} %get-tuple-element.549, f32[512,512]{0,1:T(8,128)S(1)} %get-tuple-element.489, f32[512]{0:T(512)S(1)} %get-tuple-element.488, f32[512]{0:T(512)S(1)} %get-tuple-element.492), kind=kOutput, calls=%fused_computation.7.clone.1 | convolution fusion | flops 402980864 | bytes 1576960 | tf_op jit(solution)/shard_map/while/body/eval_jaxpr/while/body/eval_jaxpr/dot_general | solution.py:99
  86.5 2.5 %fusion.71 = f32[2,512,128]{2,1,0:T(8,128)} fusion(f32[2,512,128]{2,1,0:T(8,128)} %get-tuple-element.530, s32[]{:T(128)S(6)} %copy.26, f32[512,128]{1,0:T(8,128)S(1)} %convolution_add_fusion.5, f32[512,512]{0,1:T(8,128)S(1)} %get-tuple-element.493, f32[512,128]{1,0:T(8,128)S(1)} %get-tuple-element.548), kind=kOutput, calls=%fused_computation.6.clone.1 | convolution fusion | flops 402718720 | bytes 1835012 | tf_op jit(solution)/shard_map/while/body/eval_jaxpr/while/body/eval_jaxpr/dot_general | solution.py:100
  89.0 2.5 %fusion.70 = f32[2,512,128]{2,1,0:T(8,128)} fusion(f32[2,512,128]{2,1,0:T(8,128)} %get-tuple-element.529, s32[]{:T(128)S(6)} %copy.26, f32[512,128]{1,0:T(8,128)S(1)} %get-tuple-element.548, f32[512,512]{0,1:T(8,128)S(1)} %get-tuple-element.489, f32[512]{0:T(512)S(1)} %get-tuple-element.488, f32[512]{0:T(512)S(1)} %get-tuple-element.492), kind=kOutput, calls=%fused_computation.10.clone.1 | convolution fusion | flops 402980864 | bytes 1576964 | tf_op jit(solution)/shard_map/while/body/eval_jaxpr/while/body/eval_jaxpr/dot_general | solution.py:96
  91.5 1.9 fusion.66
  93.5 1.0 fusion.65
  94.5 0.2 fusion.68
  94.7 1.2 fusion.67
  96.0 2.8 %convolution_add_fusion.5 = f32[512,128]{1,0:T(8,128)S(1)} fusion(f32[512,128]{1,0:T(8,128)} %get-tuple-element.549, f32[512,512]{0,1:T(8,128)S(1)} %get-tuple-element.489, f32[512]{0:T(512)S(1)} %get-tuple-element.488, f32[512]{0:T(512)S(1)} %get-tuple-element.492), kind=kOutput, calls=%fused_computation.7.clone.1 | convolution fusion | flops 402980864 | bytes 1576960 | tf_op jit(solution)/shard_map/while/body/eval_jaxpr/while/body/eval_jaxpr/dot_general | solution.py:99
  98.8 2.5 %fusion.71 = f32[2,512,128]{2,1,0:T(8,128)} fusion(f32[2,512,128]{2,1,0:T(8,128)} %get-tuple-element.530, s32[]{:T(128)S(6)} %copy.26, f32[512,128]{1,0:T(8,128)S(1)} %convolution_add_fusion.5, f32[512,512]{0,1:T(8,128)S(1)} %get-tuple-element.493, f32[512,128]{1,0:T(8,128)S(1)} %get-tuple-element.548), kind=kOutput, calls=%fused_computation.6.clone.1 | convolution fusion | flops 402718720 | bytes 1835012 | tf_op jit(solution)/shard_map/while/body/eval_jaxpr/while/body/eval_jaxpr/dot_general | solution.py:100
  101.3 2.5 %fusion.70 = f32[2,512,128]{2,1,0:T(8,128)} fusion(f32[2,512,128]{2,1,0:T(8,128)} %get-tuple-element.529, s32[]{:T(128)S(6)} %copy.26, f32[512,128]{1,0:T(8,128)S(1)} %get-tuple-element.548, f32[512,512]{0,1:T(8,128)S(1)} %get-tuple-element.489, f32[512]{0:T(512)S(1)} %get-tuple-element.488, f32[512]{0:T(512)S(1)} %get-tuple-element.492), kind=kOutput, calls=%fused_computation.10.clone.1 | convolution fusion | flops 402980864 | bytes 1576964 | tf_op jit(solution)/shard_map/while/body/eval_jaxpr/while/body/eval_jaxpr/dot_general | solution.py:96
  103.8 0.0 all-gather.5.cloned.1.call-update
  103.9 0.0 all-gather.3.cloned.1.call-start
  103.9 0.7 all-gather.3.cloned.1.call-update
  104.7 8.8 %all_gather.36 = f32[8,1,1024]{2,1,0:T(1,128)S(1)} all-gather(f32[1,1,1024]{2,1,0:T(1,128)S(1)} %all_gather_reshape.16), channel_id=1, replica_groups=mesh['pb'=4,'ka'=8] {'ka'}, dimensions={0}, use_global_device_ids=true | all-gather | bytes 36864 | tf_op jit(solution)/shard_map/all_gather | solution.py:8
  113.5 0.0 copy-start
  113.5 8.6 %all_gather.35 = f32[8,1,1024]{2,1,0:T(1,128)S(1)} all-gather(f32[1,1,1024]{2,1,0:T(1,128)S(1)} %all_gather_reshape.15), channel_id=1, replica_groups=mesh['pb'=4,'ka'=8] {'ka'}, dimensions={0}, use_global_device_ids=true | all-gather | bytes 36864 | tf_op jit(solution)/shard_map/all_gather | solution.py:8
  122.1 0.0 copy-start.1
  122.1 9.0 %all_gather.39 = f32[8,1,1024]{2,1,0:T(1,128)S(1)} all-gather(f32[1,1,1024]{2,1,0:T(1,128)S(1)} %all_gather_reshape.19), channel_id=1, replica_groups=mesh['pb'=4,'ka'=8] {'ka'}, dimensions={0}, use_global_device_ids=true | all-gather | bytes 36864 | tf_op jit(solution)/shard_map/all_gather | solution.py:8
  131.1 0.0 copy-start.2
  131.1 8.4 %all-gather.5.cloned.1.call-done = f32[8,1,1024,128]{3,2,1,0:T(8,128)} async-done(((f32[1,1,1024,128]{3,2,1,0:T(8,128)}), f32[8,1,1024,128]{3,2,1,0:T(8,128)}) %all-gather.5.cloned.1.call-update) | async-done | bytes 4194320 | tf_op jit(solution)/shard_map/all_gather | solution.py:8
  139.5 4.1 %slice.48 = f32[7,1,1024,128]{3,2,1,0:T(8,128)} slice(f32[8,1,1024,128]{3,2,1,0:T(8,128)} %all-gather.5.cloned.1.call-done), slice={[1:8], [0:1], [0:1024], [0:128]} | slice | bytes 7340032 | tf_op jit(solution)/shard_map/slice | solution.py:10
  143.6 1.1 slice_bitcast_fusion
  144.7 0.0 copy-done
  144.7 0.0 copy-done.1
  144.7 0.0 copy-done.2
  144.7 33.3 %all-gather.3.cloned.1.call-done = f32[8,1,1024,128]{3,2,1,0:T(8,128)} async-done(((f32[1,1,1024,128]{3,2,1,0:T(8,128)}), f32[8,1,1024,128]{3,2,1,0:T(8,128)}) %all-gather.3.cloned.1.call-update) | async-done | bytes 4194320 | tf_op jit(solution)/shard_map/all_gather | solution.py:8
  178.0 0.0 slice-start
  178.0 0.0 slice-start.1
  178.0 0.0 slice-start.2
  178.0 1.1 slice_bitcast_fusion.1
  179.1 4.1 %slice.47 = f32[7,1,1024,128]{3,2,1,0:T(8,128)} slice(f32[8,1,1024,128]{3,2,1,0:T(8,128)} %all-gather.3.cloned.1.call-done), slice={[1:8], [0:1], [0:1024], [0:128]} | slice | bytes 7340032 | tf_op jit(solution)/shard_map/slice | solution.py:10
  183.2 0.0 slice-done
  183.2 0.0 slice-done.1
  183.2 0.0 slice-done.2
  183.2 12.5 %while.54 = (s32[]{:T(128)}, f32[1,1024]{1,0:T(1,128)S(1)}, f32[1,1024]{1,0:T(1,128)S(1)}, f32[1,1024,128]{2,1,0:T(8,128)S(1)}, f32[1,1024,128]{2,1,0:T(8,128)S(...) while((s32[]{:T(128)}, f32[1,1024]{1,0:T(1,128)S(1)}, ...), condition=%wide.region_6.7_spmd, body=%wide.region_5.6_spmd.sunk | while | flops 795650 | bytes 3207305 | solution.py:11
  183.2 1.7 fusion.74
  185.0 1.7 fusion.74
  186.8 1.7 fusion.74
  188.6 1.7 fusion.74
  190.4 1.7 fusion.74
  192.2 1.7 fusion.74
  194.0 1.7 fusion.74
  195.7 0.7 multiply_subtract_fusion
  (43 shorter events, 0.8 us)
Async XLA Ops:
  7.2 132.4 %all-gather.5.cloned.1.call-start = ((), (), s32[]{:S(2)}) async-start(), calls=%async_computation.1 | async-start | bytes 4718592 | tf_op jit(solution)/shard_map/all_gather | solution.py:8
  7.2 38.3 %collective-permute-start = (f32[1,128,128]{2,1,0:T(8,128)}, f32[1,128,128]{2,1,0:T(8,128)S(1)}, u32[]{:S(2)}, u32[]{:S(2)}) collective-permute-start(f32[1,128,128]{2,1,0:T(8,128)} %param.12), channel_id=1, source_target_pairs={{0,8},{8,16},{16,24},{24,0},{1,9},{9,17},{17,25},{25,1},{2,10},{10... | collective-permute-start | bytes 196616 | tf_op jit(solution)/shard_map/ppermute | solution.py:53
  45.5 15.1 %collective-permute-start.1 = (f32[1,128,128]{2,1,0:T(8,128)S(1)}, f32[1,128,128]{2,1,0:T(8,128)S(1)}, u32[]{:S(2)}, u32[]{:S(2)}) collective-permute-start(f32[1,128,128]{2,1,0:T(8,128)S(1)} %collective-permute-done), channel_id=1, source_target_pairs={{0,8},{8,16},{16,24},{24,0},{1,9},{9,17},{17,25},{25,1},{2,10},{10... | collective-permute-start | bytes 196616 | tf_op jit(solution)/shard_map/ppermute | solution.py:53
  60.6 16.8 %collective-permute-start.2 = (f32[1,128,128]{2,1,0:T(8,128)S(1)}, f32[1,128,128]{2,1,0:T(8,128)S(1)}, u32[]{:S(2)}, u32[]{:S(2)}) collective-permute-start(f32[1,128,128]{2,1,0:T(8,128)S(1)} %collective-permute-done.1), channel_id=1, source_target_pairs={{0,8},{8,16},{16,24},{24,0},{1,9},{9,17},{17,25},{25,1},{2,10},{10... | collective-permute-start | bytes 196616 | tf_op jit(solution)/shard_map/ppermute | solution.py:53
  103.9 74.1 %all-gather.3.cloned.1.call-start = ((), (), s32[]{:S(2)}) async-start(), calls=%async_computation | async-start | bytes 4718592 | tf_op jit(solution)/shard_map/all_gather | solution.py:8
  113.5 31.2 %copy-start = (f32[8,1,1024]{2,1,0:T(1,128)}, f32[8,1,1024]{2,1,0:T(1,128)S(1)}, u32[]{:S(2)}) copy-start(f32[8,1,1024]{2,1,0:T(1,128)S(1)} %all_gather.36) | copy-start | bytes 98308
  122.1 22.6 %copy-start.1 = (f32[8,1,1024]{2,1,0:T(1,128)}, f32[8,1,1024]{2,1,0:T(1,128)S(1)}, u32[]{:S(2)}) copy-start(f32[8,1,1024]{2,1,0:T(1,128)S(1)} %all_gather.35) | copy-start | bytes 98308
  131.1 13.6 %copy-start.2 = (f32[8,1,1024]{2,1,0:T(1,128)}, f32[8,1,1024]{2,1,0:T(1,128)S(1)}, u32[]{:S(2)}) copy-start(f32[8,1,1024]{2,1,0:T(1,128)S(1)} %all_gather.39) | copy-start | bytes 98308
  178.0 5.2 %slice-start = ((f32[8,1,1024]{2,1,0:T(1,128)}), f32[7,1,1024]{2,1,0:T(1,128)S(1)}, s32[]{:S(2)}) async-start(f32[8,1,1024]{2,1,0:T(1,128)} %copy-done), calls=%async_computation.2 | async-start | bytes 57344 | tf_op jit(solution)/shard_map/slice | solution.py:10
  178.0 5.2 %slice-start.1 = ((f32[8,1,1024]{2,1,0:T(1,128)}), f32[7,1,1024]{2,1,0:T(1,128)S(1)}, s32[]{:S(2)}) async-start(f32[8,1,1024]{2,1,0:T(1,128)} %copy-done.1), calls=%async_computation.3 | async-start | bytes 57344 | tf_op jit(solution)/shard_map/slice | solution.py:10
  178.0 5.2 %slice-start.2 = ((f32[8,1,1024]{2,1,0:T(1,128)}), f32[7,1,1024]{2,1,0:T(1,128)S(1)}, s32[]{:S(2)}) async-start(f32[8,1,1024]{2,1,0:T(1,128)} %copy-done.2), calls=%async_computation.4 | async-start | bytes 57344 | tf_op jit(solution)/shard_map/slice | solution.py:10
Sparse Core Ops, SparseCore 0:
  104.0 35.4 all-gather.4
  141.4 36.5 all-gather.2
